TPU v7x, 32 devices: a whole 2x2x4 slice. The times are simulated.
32 devices in a mesh: row: 4 (over x, core), col: 8 (over z, y).
Axes of the slice: x: 2, y: 2, z: 4, core: 2. Of those that a mesh axis runs over, the one named last changes fastest.
Arguments:
- tokens: bfloat16 [16384, 1024], P(('row', 'col')), may hold values from -6 to 6
- expert_ids: int32 [16384, 1], P(('row', 'col')), may hold values from 0 to 31; in each aligned block of 512 rows (0 to 511, 512 to 1023, ...) at most 32 rows name the same one
- gate_prob: float32 [16384], P(('row', 'col')), may hold values from 0.25 to 1
- norm_gain: float32 [1024], replicated, may hold values from 0.1 to 1.9
- weight_in: bfloat16 [32, 1024, 4096], P(('row', 'col')), may hold values from -0.1875 to 0.1875
- weight_out: bfloat16 [32, 4096, 1024], P(('row', 'col')), may hold values from -0.09375 to 0.09375
Outputs:
- mixed: bfloat16 [16384, 1024], P(('row', 'col'))
- routed: int32 [32], P(('row', 'col'))
Inputs may be any that keep to these rules, and one draw needn't show every extreme that they name: `expert_ids`: among the 512 tokens of one device no expert is chosen more than 32 times; some expert is chosen exactly 32 times by some device's tokens.
All inputs are finite; a program needn't handle non-finite values.
Results may differ from a plain program's by a relative error of at most 0.001.
The roundings to bfloat16 on the way count: a program that leaves them out, or rounds other values in their place, can miss the bound.
Values may be sent and summed in bfloat16 or wider, within the bound.
A program may use at most 64 MiB of HBM per device.

v0:
```python
import jax
import jax.numpy as jnp
from jax import lax
from jax.sharding import PartitionSpec as P


def slot_rank(block_ids):
    count = block_ids.shape[0]
    same = block_ids[:, None] == block_ids[None, :]
    earlier = (
        jnp.arange(count, dtype=jnp.int32)[None, :] < jnp.arange(count, dtype=jnp.int32)[:, None]
    )
    return jnp.sum((same & earlier).astype(jnp.int32), axis=1)


def run_expert(received, first, second):
    lead = received.shape[:-1]
    width = received.shape[-1]
    flat_rows = received.reshape(-1, width)
    hidden = jnp.maximum(jnp.dot(flat_rows, first, preferred_element_type=jnp.float32), 0.0).astype(
        jnp.bfloat16
    )
    answer = jnp.dot(hidden, second, preferred_element_type=jnp.float32).astype(jnp.bfloat16)
    return answer.reshape(lead + (width,))


def on_device(tokens, expert_ids, gate_prob, norm_gain, weight_in, weight_out):
    tok_rows, width = tokens.shape
    row_count = lax.axis_size("row")
    col_count = lax.axis_size("col")
    experts = row_count * col_count
    capacity = 2 * tok_rows // experts
    local_ids = expert_ids[:, 0]
    within = slot_rank(local_ids)
    placed = local_ids * capacity + within
    wide = tokens.astype(jnp.float32)
    scale = lax.rsqrt(jnp.mean(wide * wide, axis=1, keepdims=True) + 1e-06)
    normed = (wide * scale * norm_gain[None, :]).astype(jnp.bfloat16)
    matches = (local_ids[:, None] == jnp.arange(experts, dtype=jnp.int32)[None, :]).astype(
        jnp.float32
    )
    counts = jnp.sum(matches, axis=0)
    routed = lax.psum_scatter(counts, ("row", "col"), scatter_dimension=0, tiled=True).astype(
        jnp.int32
    )
    table = (placed[None, :] == jnp.arange(experts * capacity, dtype=jnp.int32)[:, None]).astype(
        jnp.bfloat16
    )
    outgoing = jnp.dot(table, normed, preferred_element_type=jnp.float32).astype(jnp.bfloat16)
    first = weight_in[0]
    second = weight_out[0]
    answers = run_expert(
        lax.all_to_all(
            outgoing.reshape(experts, capacity, width),
            ("row", "col"),
            split_axis=0,
            concat_axis=0,
            tiled=True,
        ),
        first,
        second,
    )
    returned = lax.all_to_all(answers, ("row", "col"), split_axis=0, concat_axis=0, tiled=True)
    returned = returned.reshape(experts * capacity, width)
    back = jnp.einsum("st,sd->td", table, returned, preferred_element_type=jnp.float32)
    mixed = (wide + gate_prob[:, None] * back).astype(jnp.bfloat16)
    return (mixed, routed)


def solution(mesh):
    return jax.shard_map(
        on_device,
        mesh=mesh,
        in_specs=(
            P(("row", "col"), None),
            P(("row", "col"), None),
            P(("row", "col")),
            P(),
            P(("row", "col"), None, None),
            P(("row", "col"), None, None),
        ),
        out_specs=(P(("row", "col"), None), P(("row", "col"))),
        check_vma=False,
    )
```

profile of v0, /device:TPU:0, one launch (start us, length us, event | category | flops | bytes accessed | tf_op | source)
XLA Modules:
  0.0 164.6 jit_solution(3077922862869271912)
XLA Ops:
  0.6 1.0 convert_reduce_fusion
  1.6 0.7 multiply_add_fusion
  2.3 1.5 fusion.5
  3.8 2.6 %fusion.16 = bf16[1024,1024]{1,0:T(8,128)(2,1)S(1)} fusion(bf16[512,1024]{1,0:T(8,128)(2,1)} %param.6, f32[1024]{0:T(1024)} %param.9, f32[512]{0:T(512)S(1)} %add_rsqrt_fusion, s32[512]{0:T(512)S(1)} %multiply_add_fusion), kind=kOutput, calls=%fused_computation.15 | convolution fusion | flops 1077411840 | bytes 3153920 | tf_op jit(solution)/shard_map/dot_general | solution.py:49
  6.5 57.1 %all_to_all.10 = bf16[32,32,1024]{2,1,0:T(8,128)(2,1)S(1)} all-to-all(bf16[32,32,1024]{2,1,0:T(8,128)(2,1)S(1)} %bitcast.21), channel_id=1, replica_groups=mesh['row'=4,'col'=8] {'row','col'}, dimensions={0} | all-to-all | bytes 4194304 | tf_op jit(solution)/shard_map/all_to_all | solution.py:53
  63.5 24.6 %fusion.11 = bf16[1024,1024]{1,0:T(8,128)(2,1)} fusion(bf16[1,4096,1024]{2,1,0:T(8,128)(2,1)} %param.11, bf16[1024,1024]{1,0:T(8,128)(2,1)S(1)} %bitcast.22, bf16[1,1024,4096]{2,1,0:T(8,128)(2,1)} %param.10), kind=kOutput, calls=%fused_computation.14 | convolution fusion | flops 17189306368 | bytes 20971520 | tf_op jit(solution)/shard_map/dot_general | solution.py:23
  88.2 0.0 copy-start.1
  88.2 0.0 copy-start
  88.2 0.0 copy-start.2
  88.2 2.9 %all-to-all-start.1 = ((bf16[32,32,1024]{2,1,0:T(8,128)(2,1)}), bf16[32,32,1024]{2,1,0:T(8,128)(2,1)S(1)}, u32[]{:S(2)}, u32[]{:S(2)}) async-start(bf16[32,32,1024]{2,1,0:T(8,128)(2,1)} %bitcast.20), calls=%async_computation.1 | async-start | bytes 4194304 | tf_op jit(solution)/shard_map/all_to_all | solution.py:63
  91.0 0.0 copy-done.1
  91.0 0.1 convert_reduce_fusion.1
  91.2 68.8 %all-reduce = f32[32]{0:T(128)S(1)} all-reduce(f32[32]{0:T(128)S(1)} %convert_reduce_fusion.1), channel_id=2, replica_groups=mesh['row'=4,'col'=8] {'row','col'}, use_global_device_ids=true, to_apply=%region_3.0.clone | all-reduce | flops 32 | bytes 256
  160.0 0.6 dynamic-slice
  161.2 0.0 all-to-all-done.1
  161.2 0.0 copy-done
  161.2 0.0 copy-done.2
  161.2 2.3 %fusion.8 = bf16[512,1024]{1,0:T(8,128)(2,1)} fusion(bf16[512,1024]{1,0:T(8,128)(2,1)S(1)} %copy-done, bf16[1024,1024]{1,0:T(8,128)(2,1)S(1)} %bitcast.19, s32[512]{0:T(512)S(1)} %multiply_add_fusion, f32[512]{0:T(512)S(1)} %copy-done.2), kind=kOutput, calls=%fused_computation.10 | convolution fusion | flops 1076363264 | bytes 4198400 | tf_op jit(solution)/shard_map/st,sd->td/dot_general | solution.py:65
  (1 shorter events, 0.0 us)
Async XLA Ops:
  88.2 2.9 %copy-start.1 = (s32[512,1]{0,1:T(1,128)S(1)}, s32[512,1]{0,1:T(1,128)}, u32[]{:S(2)}) copy-start(s32[512,1]{0,1:T(1,128)} %param.7) | copy-start | bytes 6148
  88.2 73.1 %copy-start = (bf16[512,1024]{1,0:T(8,128)(2,1)S(1)}, bf16[512,1024]{1,0:T(8,128)(2,1)}, u32[]{:S(2)}) copy-start(bf16[512,1024]{1,0:T(8,128)(2,1)} %param.6) | copy-start | bytes 3145732
  88.2 73.1 %copy-start.2 = (f32[512]{0:T(512)S(1)}, f32[512]{0:T(512)}, u32[]{:S(2)}) copy-start(f32[512]{0:T(512)} %param.8) | copy-start | bytes 6148
  88.2 73.0 %all-to-all-start.1 = ((bf16[32,32,1024]{2,1,0:T(8,128)(2,1)}), bf16[32,32,1024]{2,1,0:T(8,128)(2,1)S(1)}, u32[]{:S(2)}, u32[]{:S(2)}) async-start(bf16[32,32,1024]{2,1,0:T(8,128)(2,1)} %bitcast.20), calls=%async_computation.1 | async-start | bytes 4194304 | tf_op jit(solution)/shard_map/all_to_all | solution.py:63
where the time goes:
time: 165 us
  blocking collectives  126 us (76%)
  matrix products  29.5 us (18%)
  other arithmetic  3.32 us (2%)
  starting transfers between devices  2.86 us (2%)
  between operations  2.47 us (1%)
    unnamed x1, blocking collectives  68.8 us
    all_to_all x1, blocking collectives, on_device(): lax.all_to_all(outgoing.reshape(experts, capacity, width), ('row', 'col')...  57.1 us
    dot_general x1, matrix products, run_expert(): jnp.dot(hidden, second, preferred_element_type=jnp.float32)  24.6 us
  transfers between devices with their start and end apart: 1, of which 0 were waited for; matrix products, arithmetic and copies ran while one was open for 0% of the time, Pallas kernels for 0%

commit v1 on v0

v1 whole, which is shorter than its diff:
```python
import functools

import jax
import jax.numpy as jnp
from jax import lax
from jax.experimental import pallas as pl
from jax.experimental.pallas import tpu as pltpu
from jax.sharding import PartitionSpec as P

MESH = pl.DeviceIdType.MESH


def bit_xor(a, b, size):
    out, unit = 0, 1
    while unit < size:
        out = out + lax.rem(lax.div(a, unit) + lax.div(b, unit), 2) * unit
        unit *= 2
    return out


def kernel(
    rows, cols, cap, groups, ff_tile, out_tile,
    tokens_ref, ids_col_ref, ids_row_ref, gain_ref, first_hbm, second_hbm,
    back_ref, routed_ref,
    first, second, normed, outgoing, received, answers, returned, hidden, total,
    counts, counts_in, placed_col,
    weight_sem, send_sem, recv_sem, ret_sem, count_sem,
):
    n = rows * cols
    tok_rows, width = tokens_ref.shape
    lanes = counts.shape[1]
    per = n // groups
    span = per * cap
    my_row, my_col = lax.axis_index("row"), lax.axis_index("col")
    me = my_row * cols + my_col

    def partner(place):
        q = n - 1 - place
        return (
            bit_xor(my_row, lax.rem(q, rows), rows),
            bit_xor(my_col, lax.div(q, rows), cols),
        )

    barrier = pltpu.get_barrier_semaphore()

    @pl.loop(0, n - 1)
    def _(place):
        pl.semaphore_signal(barrier, inc=1, device_id=partner(place), device_id_type=MESH)

    load_first = pltpu.make_async_copy(first_hbm.at[0], first, weight_sem.at[0])
    load_second = pltpu.make_async_copy(second_hbm.at[0], second, weight_sem.at[1])
    load_first.start()
    load_second.start()

    def slot_of(ids, within):
        offset = jnp.bitwise_xor(ids, me)
        q = (offset % cols) * rows + offset // cols
        return (n - 1 - q) * cap + within

    ids_row = ids_row_ref[...]
    ids_col = ids_col_ref[...]
    at_row = lax.broadcasted_iota(jnp.int32, (tok_rows, tok_rows), 0)
    at_col = lax.broadcasted_iota(jnp.int32, (tok_rows, tok_rows), 1)
    hot_row = lax.broadcasted_iota(jnp.int32, (lanes, tok_rows), 0) == ids_row
    before = jnp.where(at_row < at_col, 1.0, 0.0).astype(jnp.bfloat16)
    earlier = jnp.dot(
        jnp.where(hot_row, 1.0, 0.0).astype(jnp.bfloat16), before, preferred_element_type=jnp.float32
    )
    within_row = jnp.sum(jnp.where(hot_row, earlier, 0.0), axis=0, keepdims=True)
    placed_row = slot_of(ids_row, within_row.astype(jnp.int32))

    wide = tokens_ref[...].astype(jnp.float32)
    scale = lax.rsqrt(jnp.mean(wide * wide, axis=1, keepdims=True) + 1e-06)
    normed[...] = (wide * scale * gain_ref[...]).astype(jnp.bfloat16)

    def as_blocks(values):
        return values.reshape(per, cap, width).astype(jnp.bfloat16)

    def as_rows(ref, g):
        blocks = ref[pl.ds(g * per, per)]
        if cap % 16 == 0:
            return blocks.reshape(span, width)
        return blocks.astype(jnp.float32).reshape(span, width).astype(jnp.bfloat16)

    def exchange(source, target, sem, out_sem, g):
        @pl.loop(0, per)
        def _(i):
            place = g * per + i

            @pl.when(place < n - 1)
            def _():
                pltpu.make_async_remote_copy(
                    src_ref=source.at[place],
                    dst_ref=target.at[place],
                    send_sem=out_sem,
                    recv_sem=sem.at[g],
                    device_id=partner(place),
                    device_id_type=MESH,
                ).start()

            @pl.when(place == n - 1)
            def _():
                pltpu.make_async_copy(source.at[n - 1], target.at[n - 1], sem.at[g]).start()

    def wait_group(target, sem, g):
        whole = target.at[pl.ds(g * per, per)]
        pltpu.make_async_copy(whole, whole, sem.at[g]).wait()

    @pl.loop(0, groups)
    def _(g):
        slot = lax.broadcasted_iota(jnp.int32, (span, tok_rows), 0) + g * span
        table = jnp.where(slot == placed_row, 1.0, 0.0).astype(jnp.bfloat16)
        outgoing[pl.ds(g * per, per)] = as_blocks(
            jnp.dot(table, normed[...], preferred_element_type=jnp.float32)
        )

        @pl.when(g == 0)
        def _():
            pl.semaphore_wait(barrier, n - 1)

        exchange(outgoing, received, recv_sem, send_sem.at[0], g)

    hot_col = lax.broadcasted_iota(jnp.int32, (tok_rows, lanes), 1) == ids_col
    ones_col = jnp.where(hot_col, 1.0, 0.0)
    counts[...] = jnp.sum(ones_col, axis=0, keepdims=True)
    after = jnp.where(at_col < at_row, 1.0, 0.0).astype(jnp.bfloat16)
    earlier_col = jnp.dot(after, ones_col.astype(jnp.bfloat16), preferred_element_type=jnp.float32)
    within_col = jnp.sum(jnp.where(hot_col, earlier_col, 0.0), axis=1, keepdims=True)
    placed_col[...] = slot_of(ids_col, within_col.astype(jnp.int32))
    total[...] = jnp.zeros_like(total)

    @pl.loop(0, n - 1)
    def _(place):
        pltpu.make_async_remote_copy(
            src_ref=counts,
            dst_ref=counts_in.at[place],
            send_sem=send_sem.at[2],
            recv_sem=count_sem,
            device_id=partner(place),
            device_id_type=MESH,
        ).start()

    load_first.wait()
    load_second.wait()

    @pl.loop(0, groups)
    def _(step):
        g = lax.rem(step + groups - 1, groups)
        wait_group(received, recv_sem, g)
        slab = as_rows(received, g)

        @pl.loop(0, first.shape[1] // ff_tile)
        def _(i):
            part = pl.ds(pl.multiple_of(i * ff_tile, ff_tile), ff_tile)
            grown = jnp.dot(slab, first[:, part], preferred_element_type=jnp.float32)
            hidden[:, part] = jnp.maximum(grown, 0.0).astype(jnp.bfloat16)

        @pl.loop(0, width // out_tile)
        def _(i):
            part = pl.ds(pl.multiple_of(i * out_tile, out_tile), out_tile)
            made = jnp.dot(hidden[...], second[:, part], preferred_element_type=jnp.float32)
            answers[pl.ds(g * per, per), :, part] = made.reshape(per, cap, out_tile).astype(
                jnp.bfloat16
            )

        exchange(answers, returned, ret_sem, send_sem.at[1], g)

    arrived = counts_in.at[pl.ds(0, n - 1)]
    pltpu.make_async_copy(arrived, arrived, count_sem).wait()
    sums = jnp.sum(counts_in[pl.ds(0, n - 1)], axis=0) + counts[...]
    mine = lax.broadcasted_iota(jnp.int32, (1, lanes), 1) == me
    routed_ref[0] = jnp.sum(jnp.where(mine, sums, 0.0)).astype(jnp.int32)

    @pl.loop(0, groups)
    def _(step):
        g = lax.rem(step + groups - 1, groups)
        wait_group(returned, ret_sem, g)
        slot = lax.broadcasted_iota(jnp.int32, (tok_rows, span), 1) + g * span
        table = jnp.where(slot == placed_col[...], 1.0, 0.0).astype(jnp.bfloat16)
        total[...] += jnp.dot(table, as_rows(returned, g), preferred_element_type=jnp.float32)

    back_ref[...] = total[...].astype(jnp.bfloat16)

    sent = outgoing.at[pl.ds(0, n - 1)]
    pltpu.make_async_copy(sent, sent, send_sem.at[0]).wait()
    pltpu.make_async_copy(sent, sent, send_sem.at[1]).wait()
    pltpu.make_async_copy(arrived, arrived, send_sem.at[2]).wait()


def on_device(rows, cols, tokens, expert_ids, gate_prob, norm_gain, weight_in, weight_out):
    tok_rows, width = tokens.shape
    hidden_width = weight_in.shape[2]
    n = rows * cols
    cap = 2 * tok_rows // n
    lanes = -(-n // 128) * 128
    per = max(1, min(n, 256 // cap))
    groups = n // per
    vmem = pl.BlockSpec(memory_space=pltpu.VMEM)
    hbm = pl.BlockSpec(memory_space=pl.ANY)
    block = pltpu.VMEM((n, cap, width), jnp.bfloat16)
    back, routed = pl.pallas_call(
        functools.partial(kernel, rows, cols, cap, groups, min(512, hidden_width), min(256, width)),
        out_shape=(
            jax.ShapeDtypeStruct((tok_rows, width), jnp.bfloat16),
            jax.ShapeDtypeStruct((1,), jnp.int32),
        ),
        in_specs=[vmem, vmem, vmem, vmem, hbm, hbm],
        out_specs=(vmem, pl.BlockSpec(memory_space=pltpu.SMEM)),
        scratch_shapes=[
            pltpu.VMEM((width, hidden_width), jnp.bfloat16),
            pltpu.VMEM((hidden_width, width), jnp.bfloat16),
            pltpu.VMEM((tok_rows, width), jnp.bfloat16),
            block, block, block, block,
            pltpu.VMEM((per * cap, hidden_width), jnp.bfloat16),
            pltpu.VMEM((tok_rows, width), jnp.float32),
            pltpu.VMEM((1, lanes), jnp.float32),
            pltpu.VMEM((n, 1, lanes), jnp.float32),
            pltpu.VMEM((tok_rows, 1), jnp.int32),
            pltpu.SemaphoreType.DMA((2,)),
            pltpu.SemaphoreType.DMA((3,)),
            pltpu.SemaphoreType.DMA((groups,)),
            pltpu.SemaphoreType.DMA((groups,)),
            pltpu.SemaphoreType.DMA,
        ],
        compiler_params=pltpu.CompilerParams(
            collective_id=0, has_side_effects=True, vmem_limit_bytes=56 * 1024 * 1024
        ),
    )(
        tokens,
        expert_ids,
        expert_ids.reshape(1, tok_rows),
        norm_gain.reshape(1, width),
        weight_in,
        weight_out,
    )
    wide = tokens.astype(jnp.float32)
    mixed = (wide + gate_prob[:, None] * back.astype(jnp.float32)).astype(jnp.bfloat16)
    return (mixed, routed)


def solution(mesh):
    return jax.shard_map(
        functools.partial(on_device, mesh.shape["row"], mesh.shape["col"]),
        mesh=mesh,
        in_specs=(
            P(("row", "col"), None),
            P(("row", "col"), None),
            P(("row", "col")),
            P(),
            P(("row", "col"), None, None),
            P(("row", "col"), None, None),
        ),
        out_specs=(P(("row", "col"), None), P(("row", "col"))),
        check_vma=False,
    )
```

time: 165 us -> 113 us (0.68)
  blocking collectives: 126 us -> 0 us
  Pallas kernels: 0 us -> 106 us
  matrix products: 29.5 us -> 0 us
  starting transfers between devices: 2.86 us -> 0 us
    pallas_call x0 -> x1, Pallas kernels: none -> 106 us  [on_device(): pl.pallas_call(functools.partial(kernel, rows, cols, cap, groups, min(512...]
    unnamed x1 -> x0, blocking collectives: 68.8 us -> none
    all_to_all x1 -> x0, blocking collectives: 57.1 us -> none  [on_device(): lax.all_to_all(outgoing.reshape(experts, capacity, width), ('row', 'col')...]
    dot_general x3 -> x0, matrix products: 29.5 us -> none  [the longest x1 24.6 us: run_expert(): jnp.dot(hidden, second, preferred_element_type=jnp.float32)]
    all_to_all x1 -> x0, starting transfers between devices: 2.86 us -> none  [on_device(): lax.all_to_all(answers, ('row', 'col'), split_axis=0, concat_axis=0, tile...]
    reduce_sum x3 -> x0, other arithmetic: 2.62 us -> none  [the longest x1 1.5 us: on_device(): scale = lax.rsqrt(jnp.mean(wide * wide, axis=1, keepdims=True) + 1e-06)]
    convert_element_type x0 -> x1, other arithmetic: none -> 2.57 us  [on_device(): (wide + gate_prob[:, None] * back.astype(jnp.float32)).astype(jnp.bfloat16)]
  transfers between devices with their start and end apart: 1 -> 0, of which waited for: 0 -> 0; matrix products, arithmetic and copies ran while one was open for 0% -> 0% of each run, Pallas kernels for 0% -> 0%
where the time goes in v1:
time: 113 us
  Pallas kernels  106 us (94%)
  other arithmetic  2.57 us (2%)
  between operations  2.41 us (2%)
  local copies, waits for them, and re-layouts  1.54 us (1%)
    pallas_call x1, Pallas kernels, on_device(): pl.pallas_call(functools.partial(kernel, rows, cols, cap, groups, min(512...  106 us
    convert_element_type x1, other arithmetic, on_device(): (wide + gate_prob[:, None] * back.astype(jnp.float32)).astype(jnp.bfloat16)  2.57 us

profile of v1, /device:TPU:0, one launch (start us, length us, event | category | flops | bytes accessed | tf_op | source)
XLA Modules:
  0.0 112.6 jit_solution(17311724722374856445)
XLA Ops:
  0.6 1.5 %copy.8.ids_col_ref = s32[512,1]{1,0:T(8,128)} copy(s32[512,1]{0,1:T(1,128)} %param.7) | data formatting | bytes 4096 | tf_op args[1]
  2.2 0.0 copy-start
  2.2 0.0 copy-start.1
  2.2 106.1 %shard_map.77 = (bf16[512,1024]{1,0:T(8,128)(2,1)}, s32[1]{0:T(128)}) custom-call(bf16[512,1024]{1,0:T(8,128)(2,1)} %tokens_ref.1, s32[512,1]{1,0:T(8,128)} %copy.8.ids_col_ref, s32[1,512]{1,0:T(1,128)} %bitcast.2, f32[1,1024]{1,0:T(1,128)} %bitcast.3, bf16[1,1024,4096]{2,1,0:T(8,128)(2,1)} %first_hbm.1, bf16[1,4096,1024]{2,1,0:T(8,128)(2,1)} %second_hbm.1), custom_call_target="tpu_custom_call" | custom-call | tf_op jit(solution)/shard_map/pallas_call | solution.py:201
  108.3 0.0 copy-done
  108.3 0.0 copy-done.1
  108.3 2.6 %add_convert_fusion = bf16[512,1024]{1,0:T(8,128)(2,1)} fusion(bf16[512,1024]{1,0:T(8,128)(2,1)} %get-tuple-element.4, bf16[512,1024]{1,0:T(8,128)(2,1)S(1)} %copy-done, f32[512]{0:T(512)S(1)} %copy-done.1), kind=kLoop, calls=%fused_computation | loop fusion | flops 2621440 | bytes 3147776 | tf_op jit(solution)/shard_map/convert_element_type | solution.py:237
Async XLA Ops:
  2.2 106.1 %copy-start = (bf16[512,1024]{1,0:T(8,128)(2,1)S(1)}, bf16[512,1024]{1,0:T(8,128)(2,1)}, u32[]{:S(2)}) copy-start(bf16[512,1024]{1,0:T(8,128)(2,1)} %tokens_ref.1) | copy-start | bytes 3145732
  2.2 106.1 %copy-start.1 = (f32[512]{0:T(512)S(1)}, f32[512]{0:T(512)}, u32[]{:S(2)}) copy-start(f32[512]{0:T(512)} %param.8) | copy-start | bytes 6148

commit v2 on v1

--- a/solution.py
+++ b/solution.py
@@ -20,7 +20,7 @@
 
 def kernel(
     rows, cols, cap, groups, ff_tile, out_tile,
-    tokens_ref, ids_col_ref, ids_row_ref, gain_ref, first_hbm, second_hbm,
+    tokens_ref, ids_row_ref, gain_ref, first_hbm, second_hbm,
     back_ref, routed_ref,
     first, second, normed, outgoing, received, answers, returned, hidden, total,
     counts, counts_in, placed_col,
@@ -34,6 +34,11 @@
     my_row, my_col = lax.axis_index("row"), lax.axis_index("col")
     me = my_row * cols + my_col
 
+    def turn(step):
+        if groups % 2:
+            return step
+        return lax.rem(step, 2) * (groups // 2) + lax.div(step, 2)
+
     def partner(place):
         q = n - 1 - place
         return (
@@ -58,7 +63,6 @@
         return (n - 1 - q) * cap + within
 
     ids_row = ids_row_ref[...]
-    ids_col = ids_col_ref[...]
     at_row = lax.broadcasted_iota(jnp.int32, (tok_rows, tok_rows), 0)
     at_col = lax.broadcasted_iota(jnp.int32, (tok_rows, tok_rows), 1)
     hot_row = lax.broadcasted_iota(jnp.int32, (lanes, tok_rows), 0) == ids_row
@@ -107,26 +111,28 @@
         pltpu.make_async_copy(whole, whole, sem.at[g]).wait()
 
     @pl.loop(0, groups)
-    def _(g):
+    def _(step):
+        g = turn(step)
         slot = lax.broadcasted_iota(jnp.int32, (span, tok_rows), 0) + g * span
         table = jnp.where(slot == placed_row, 1.0, 0.0).astype(jnp.bfloat16)
         outgoing[pl.ds(g * per, per)] = as_blocks(
             jnp.dot(table, normed[...], preferred_element_type=jnp.float32)
         )
 
-        @pl.when(g == 0)
+        @pl.when(step == 0)
         def _():
             pl.semaphore_wait(barrier, n - 1)
 
         exchange(outgoing, received, recv_sem, send_sem.at[0], g)
 
-    hot_col = lax.broadcasted_iota(jnp.int32, (tok_rows, lanes), 1) == ids_col
-    ones_col = jnp.where(hot_col, 1.0, 0.0)
-    counts[...] = jnp.sum(ones_col, axis=0, keepdims=True)
-    after = jnp.where(at_col < at_row, 1.0, 0.0).astype(jnp.bfloat16)
-    earlier_col = jnp.dot(after, ones_col.astype(jnp.bfloat16), preferred_element_type=jnp.float32)
-    within_col = jnp.sum(jnp.where(hot_col, earlier_col, 0.0), axis=1, keepdims=True)
-    placed_col[...] = slot_of(ids_col, within_col.astype(jnp.int32))
+    counts[...] = lax.dot_general(
+        jnp.ones((8, tok_rows), jnp.bfloat16),
+        jnp.where(hot_row, 1.0, 0.0).astype(jnp.bfloat16),
+        (((1,), (1,)), ((), ())),
+        preferred_element_type=jnp.float32,
+    )[0:1]
+    turned = jnp.where(at_row == at_col, placed_row.astype(jnp.float32), 0.0)
+    placed_col[...] = jnp.sum(turned, axis=1, keepdims=True).astype(jnp.int32)
     total[...] = jnp.zeros_like(total)
 
     @pl.loop(0, n - 1)
@@ -145,7 +151,7 @@
 
     @pl.loop(0, groups)
     def _(step):
-        g = lax.rem(step + groups - 1, groups)
+        g = turn(lax.rem(step + groups - 1, groups))
         wait_group(received, recv_sem, g)
         slab = as_rows(received, g)
 
@@ -173,7 +179,7 @@
 
     @pl.loop(0, groups)
     def _(step):
-        g = lax.rem(step + groups - 1, groups)
+        g = turn(lax.rem(step + groups - 1, groups))
         wait_group(returned, ret_sem, g)
         slot = lax.broadcasted_iota(jnp.int32, (tok_rows, span), 1) + g * span
         table = jnp.where(slot == placed_col[...], 1.0, 0.0).astype(jnp.bfloat16)
@@ -204,7 +210,7 @@
             jax.ShapeDtypeStruct((tok_rows, width), jnp.bfloat16),
             jax.ShapeDtypeStruct((1,), jnp.int32),
         ),
-        in_specs=[vmem, vmem, vmem, vmem, hbm, hbm],
+        in_specs=[vmem, vmem, vmem, hbm, hbm],
         out_specs=(vmem, pl.BlockSpec(memory_space=pltpu.SMEM)),
         scratch_shapes=[
             pltpu.VMEM((width, hidden_width), jnp.bfloat16),
@@ -227,7 +233,6 @@
         ),
     )(
         tokens,
-        expert_ids,
         expert_ids.reshape(1, tok_rows),
         norm_gain.reshape(1, width),
         weight_in,

time: 113 us -> 112 us (level)
  local copies, waits for them, and re-layouts: 1.54 us -> 0.01 us
    unnamed x5 -> x4, local copies, waits for them, and re-layouts: 1.54 us -> 0.01 us
where the time goes in v2:
time: 112 us; the launch traced here: 111 us
  Pallas kernels  106 us (95%)
  other arithmetic  2.57 us (2%)
  between operations  2.43 us (2%)
    pallas_call x1, Pallas kernels, on_device(): pl.pallas_call(functools.partial(kernel, rows, cols, cap, groups, min(512...  106 us
    convert_element_type x1, other arithmetic, on_device(): (wide + gate_prob[:, None] * back.astype(jnp.float32)).astype(jnp.bfloat16)  2.57 us

profile of v2, /device:TPU:0, one launch (start us, length us, event | category | flops | bytes accessed | tf_op | source)
XLA Modules:
  0.0 111.5 jit_solution(132514263278800078)
XLA Ops:
  0.6 0.0 copy-start
  0.6 0.0 copy-start.1
  0.7 106.5 %shard_map.77 = (bf16[512,1024]{1,0:T(8,128)(2,1)}, s32[1]{0:T(128)}) custom-call(bf16[512,1024]{1,0:T(8,128)(2,1)} %tokens_ref.1, s32[1,512]{1,0:T(1,128)} %bitcast.3, f32[1,1024]{1,0:T(1,128)} %bitcast.2, bf16[1,1024,4096]{2,1,0:T(8,128)(2,1)} %first_hbm.1, bf16[1,4096,1024]{2,1,0:T(8,128)(2,1)} %second_hbm.1), custom_call_target="tpu_custom_call" | custom-call | tf_op jit(solution)/shard_map/pallas_call | solution.py:207
  107.1 0.0 copy-done
  107.1 0.0 copy-done.1
  107.1 2.6 %add_convert_fusion = bf16[512,1024]{1,0:T(8,128)(2,1)} fusion(bf16[512,1024]{1,0:T(8,128)(2,1)} %get-tuple-element.4, bf16[512,1024]{1,0:T(8,128)(2,1)S(1)} %copy-done, f32[512]{0:T(512)S(1)} %copy-done.1), kind=kLoop, calls=%fused_computation | loop fusion | flops 2621440 | bytes 3147776 | tf_op jit(solution)/shard_map/convert_element_type | solution.py:242
Async XLA Ops:
  0.6 106.5 %copy-start = (bf16[512,1024]{1,0:T(8,128)(2,1)S(1)}, bf16[512,1024]{1,0:T(8,128)(2,1)}, u32[]{:S(2)}) copy-start(bf16[512,1024]{1,0:T(8,128)(2,1)} %tokens_ref.1) | copy-start | bytes 3145732
  0.6 106.5 %copy-start.1 = (f32[512]{0:T(512)S(1)}, f32[512]{0:T(512)}, u32[]{:S(2)}) copy-start(f32[512]{0:T(512)} %param.8) | copy-start | bytes 6148
